TPU v7x, 32 devices: a whole 2x2x4 slice. The times are simulated.
32 devices in a mesh: rep: 8 (over z, x), tp: 4 (over y, core).
Axes of the slice: x: 2, y: 2, z: 4, core: 2. Of those that a mesh axis runs over, the one named last changes fastest.
Arguments:
- q_weight: float32 [5120, 5120], P(('rep', 'tp')), may hold values from -0.078125 to 0.078125
- key_projection_weight: float32 [1024, 5120], P(('rep', 'tp')), may hold values from -0.078125 to 0.078125
- value_projection_weight: float32 [1024, 5120], P(('rep', 'tp')), may hold values from -0.078125 to 0.078125
- tokens: bfloat16 [8192, 5120], P(('rep', 'tp')), may hold values from -6 to 6
Outputs:
- combined_query_key_value: bfloat16 [7168, 5120], P('tp')
- projected: bfloat16 [8192, 7168], P('rep', 'tp')
All inputs are finite; a program needn't handle non-finite values.
Results may differ from a plain program's by a relative error of at most 0.0049.
Values may be sent and summed in bfloat16 or wider, within the bound.
A program may use at most 192 MiB of HBM per device.

v0:
```python
import jax
import jax.numpy as jnp
from jax import lax
from jax.sharding import PartitionSpec as P


def join_blocks(blocks, q_rows, key_value_rows):
    row_width = blocks.shape[3]
    bounds = ((0, q_rows), (q_rows, key_value_rows), (q_rows + key_value_rows, key_value_rows))
    pieces = []
    for row_start, length in bounds:
        part_rows = blocks[:, :, row_start : row_start + length]
        pieces.append(jnp.transpose(part_rows, (1, 0, 2, 3)).reshape(-1, row_width))
    return jnp.concatenate(pieces, 0)


def shards(q_weight, key_projection_weight, value_projection_weight, tokens):
    rep_size = lax.axis_size("rep")
    tp_size = lax.axis_size("tp")
    per_rank = rep_size // tp_size
    q_rows = q_weight.shape[0]
    key_value_rows = key_projection_weight.shape[0]
    width = q_weight.shape[1]
    shard_rows = jnp.concatenate(
        [q_weight, key_projection_weight, value_projection_weight], 0
    ).astype(jnp.bfloat16)
    row_count = shard_rows.shape[0]
    prompts = lax.all_gather(tokens, "tp", axis=0, tiled=True)
    col_width = width // rep_size
    split_cols = shard_rows.reshape(row_count, rep_size, col_width)
    arrived = lax.all_to_all(
        lax.all_to_all(split_cols, "rep", split_axis=1, concat_axis=1, tiled=True),
        "tp",
        split_axis=1,
        concat_axis=1,
        tiled=True,
    )
    arranged = jnp.transpose(arrived.reshape(row_count, tp_size, per_rank, col_width), (1, 2, 0, 3))
    column_block = join_blocks(arranged, q_rows, key_value_rows)
    segment = lax.all_gather(column_block, "rep", axis=1, tiled=True)
    partial_sum = lax.dot_general(
        prompts, segment, (((1,), (1,)), ((), ())), preferred_element_type=jnp.float32
    )
    return (segment, partial_sum.astype(jnp.bfloat16))


def solution(mesh):
    in_specs = (
        P(("rep", "tp"), None),
        P(("rep", "tp"), None),
        P(("rep", "tp"), None),
        P(("rep", "tp"), None),
    )
    out_specs = (P("tp", None), P("rep", "tp"))
    return jax.shard_map(shards, mesh=mesh, in_specs=in_specs, out_specs=out_specs, check_vma=False)
```

profile of v0, /device:TPU:5, one launch (start us, length us, event | category | flops | bytes accessed | tf_op | source)
XLA Modules:
  0.0 513.2 jit_solution(15356739874720609581)
XLA Ops:
  7.2 0.0 all-gather.5.cloned.1.call-start
  7.2 0.7 all-gather.5.cloned.1.call-update
  7.9 0.0 copy-start
  7.9 0.0 all-gather.3.cloned.1.call-start
  8.0 1.3 convert.13
  9.3 1.1 convert.14
  10.4 0.0 copy-done
  10.5 0.2 convert.12
  10.7 0.3 copy.18
  11.0 0.3 pad_maximum_fusion
  11.3 0.3 copy.13
  11.6 57.0 %all_to_all.10 = bf16[224,8,640]{2,0,1:T(8,128)(2,1)S(1)} all-to-all(bf16[224,8,640]{2,0,1:T(8,128)(2,1)S(1)} %copy.13), channel_id=1, replica_groups=mesh['rep'=8,'tp'=4] {'rep'}, dimensions={1} | all-to-all | bytes 4587520 | tf_op jit(solution)/shard_map/all_to_all | solution.py:32
  68.5 34.2 %all_to_all.11 = bf16[224,8,640]{2,0,1:T(8,128)(2,1)S(1)} all-to-all(bf16[224,8,640]{2,0,1:T(8,128)(2,1)S(1)} %all_to_all.10), channel_id=1, replica_groups=mesh['rep'=8,'tp'=4] {'tp'}, dimensions={1} | all-to-all | bytes 4587520 | tf_op jit(solution)/shard_map/all_to_all | solution.py:31
  102.8 0.1 slice_bitcast_fusion
  102.9 0.1 copy.14
  103.1 0.1 slice_bitcast_fusion.2
  103.2 1.6 pad_maximum_fusion.1
  104.8 0.0 all-gather.3.cloned.1.call-update
  104.8 0.0 all-gather.5.cloned.1.call-done
  104.9 353.4 %all-gather.3.cloned.1.call-done = bf16[1792,5120]{1,0:T(8,128)(2,1)} async-done(((bf16[1792,640]{1,0:T(8,128)(2,1)}), bf16[1792,5120]{1,0:T(8,128)(2,1)}) %all-gather.3.cloned.1.call-update) | async-done | bytes 18350096 | tf_op jit(solution)/shard_map/all_gather | solution.py:40
  458.3 26.0 %fusion = bf16[1024,1792]{0,1:T(8,128)(2,1)} fusion(bf16[1792,5120]{1,0:T(8,128)(2,1)} %all-gather.3.cloned.1.call-done, bf16[1024,5120]{1,0:T(8,128)(2,1)} %all-gather.5.cloned.1.call-done), kind=kOutput, calls=%fused_computation.1 | convolution fusion | flops 18792316928 | bytes 32505856 | tf_op jit(solution)/shard_map/dot_general | solution.py:41
  484.3 5.9 %copy.17 = bf16[1024,1792]{1,0:T(8,128)(2,1)} copy(bf16[1024,1792]{0,1:T(8,128)(2,1)} %fusion) | data formatting | bytes 7340032
  490.2 16.1 %copy.22 = bf16[1792,5120]{1,0:T(8,128)(2,1)} copy(bf16[1792,5120]{1,0:T(8,128)(2,1)} %all-gather.3.cloned.1.call-done) | data formatting | bytes 36700160
  (4 shorter events, 0.1 us)
Async XLA Ops:
  7.2 97.7 %all-gather.5.cloned.1.call-start = ((), (), s32[]{:S(2)}) async-start(), calls=%async_computation.3 | async-start | bytes 13107200 | tf_op jit(solution)/shard_map/all_gather | solution.py:28
  7.9 2.6 copy-start
  7.9 450.3 %all-gather.3.cloned.1.call-start = ((), (), s32[]{:S(2)}) async-start(), calls=%async_computation.2 | async-start | bytes 20643840 | tf_op jit(solution)/shard_map/all_gather | solution.py:40
Sparse Core Ops, SparseCore 0:
  9.5 74.2 all-gather.4
  105.0 353.2 all-gather.2
where the time goes:
time: 515 us; the launch traced here: 513 us
  waiting for transfers between devices  354 us (69%)
  blocking collectives  91.2 us (18%)
  matrix products  26 us (5%)
  local copies, waits for them, and re-layouts  23.1 us (4%)
  between operations  14.2 us (3%)
    all_gather x1, waiting for transfers between devices, shards(): segment = lax.all_gather(column_block, 'rep', axis=1, tiled=True)  353 us
    all_to_all x1, blocking collectives, shards(): lax.all_to_all(split_cols, 'rep', split_axis=1, concat_axis=1, tiled=True)  57 us
    all_to_all x1, blocking collectives, shards(): lax.all_to_all(lax.all_to_all(split_cols, 'rep', split_axis=1, concat_axi...  34.2 us
    dot_general x1, matrix products, shards(): lax.dot_general(prompts, segment, (((1,), (1,)), ((), ())), preferred_ele...  26 us
    unnamed x7, local copies, waits for them, and re-layouts  22.4 us
  transfers between devices with their start and end apart: 2, of which 1 were waited for; matrix products, arithmetic and copies ran while one was open for 1% of the time, Pallas kernels for 0%

commit v1 on v0

v1 whole, which is shorter than its diff:
```python
import functools

import jax
import jax.numpy as jnp
from jax import lax
from jax.experimental import pallas as pl
from jax.experimental.pallas import tpu as pltpu
from jax.sharding import PartitionSpec as P

MESH = pl.DeviceIdType.MESH
LEAD = 3
Y_LAG = 5


def gather_kernel(
    rep_size, tp_size, q_rows, kv_rows,
    shard, tok, weights, prompts, relay,
    shard_buf, tok_buf, local_sem,
    part_send, part_recv, z_send, z_recv, y_send, y_recv, x_send, x_recv, tok_send, tok_recv,
):
    planes = tp_size
    columns = rep_size // planes
    half = tp_size // 2
    r, t = lax.axis_index("rep"), lax.axis_index("tp")
    plane, column = r // columns, r % columns
    side, core = t // 2, t % 2
    other = (t + half) % tp_size
    partner = t + 1 - 2 * core
    q_chunks = q_rows // kv_rows
    pieces = q_chunks + 2
    count = 2 * pieces
    shards_in_plane = tp_size * columns
    ranks = (t, other)

    def row_of(index, m):
        if m < q_chunks:
            return pl.multiple_of(index * q_rows + m * kv_rows, 8)
        base = shards_in_plane * (q_rows + (m - q_chunks) * kv_rows)
        return pl.multiple_of(base + index * kv_rows, 8)

    def in_weights(at_side, n):
        of_core = core if n < pieces else 1 - core
        return weights.at[pl.ds(row_of(column * tp_size + at_side * 2 + of_core, n % pieces), kv_rows)]

    def in_relay(n):
        return relay.at[pl.ds(n * kv_rows, kv_rows)]

    def in_shard(m):
        return shard.at[pl.ds(m * kv_rows, kv_rows)]

    def place(slot, n):
        return in_weights(side, n) if slot == 0 else in_relay(n)

    def remote(src, dst, send, recv, to_rep, to_tp):
        return pltpu.make_async_remote_copy(
            src_ref=src, dst_ref=dst, send_sem=send, recv_sem=recv,
            device_id=(to_rep, to_tp), device_id_type=MESH,
        )

    def ups(slot):
        k = ranks[slot]
        return (plane >= k) & (plane < planes - 1), (plane <= k) & (plane > 0)

    def x_sends(src, dst):
        for d in range(1, columns):
            to = plane * columns + (column + d) % columns
            remote(src, dst, x_send.at[d - 1], x_recv.at[d - 1], to, t).start()

    def forward(slot, n, src):
        up, down = ups(slot)
        dst = place(slot, n)

        @pl.when(up)
        def _():
            remote(src, dst, z_send.at[slot, 0], z_recv.at[slot, n], r + columns, t).start()

        @pl.when(down)
        def _():
            remote(src, dst, z_send.at[slot, 1], z_recv.at[slot, n], r - columns, t).start()

        if slot == 0:
            x_sends(src, dst)
        else:
            remote(src, in_weights(side, n), y_send.at[0], y_recv.at[n], r, other).start()

    def recv_wait(dst, sem):
        remote(dst, dst, x_send.at[0], sem, r, partner).wait_recv()

    def send_wait(src, sem):
        remote(src, src, sem, x_recv.at[0], r, partner).wait_send()

    def source_step(slot, n):
        @pl.when(plane == ranks[slot])
        def _():
            if n < pieces:
                forward(slot, n, in_shard(n))
            else:
                recv_wait(place(slot, n), part_recv.at[n - pieces])
                forward(slot, n, place(slot, n))

    def relay_step(slot, n):
        @pl.when(plane != ranks[slot])
        def _():
            recv_wait(place(slot, n), z_recv.at[slot, n])
            forward(slot, n, place(slot, n))

    def y_step(n):
        block = in_weights(1 - side, n)
        recv_wait(block, y_recv.at[n])
        x_sends(block, block)

    rows = tok.shape[0]

    def prompt_rows(rank):
        return prompts.at[pl.ds(pl.multiple_of(rank * rows, 8), rows)]

    handler = core == plane % 2
    load_shard = pltpu.make_async_copy(shard, shard_buf, local_sem.at[0])
    load_tok = pltpu.make_async_copy(tok, tok_buf, local_sem.at[1])
    load_shard.start()
    load_tok.start()

    @pl.when(jnp.logical_not(handler))
    def _():
        for m in range(pieces):
            @pl.when(side == plane // 2)
            def _():
                dst = weights.at[pl.ds(row_of(column * tp_size + t, m), kv_rows)]
                remote(in_shard(m), dst, part_send.at[0], part_recv.at[m], r, partner).start()

            @pl.when(side != plane // 2)
            def _():
                remote(in_shard(m), in_relay(pieces + m), part_send.at[0], part_recv.at[m], r, partner).start()

    remote(tok, prompt_rows(t), tok_send.at[0], tok_recv.at[0], r, other).start()
    remote(tok, prompt_rows(t), tok_send.at[1], tok_recv.at[1], r, partner).start()

    for n in range(LEAD):
        source_step(0, n)
        source_step(1, n)

    load_shard.wait()
    load_tok.wait()
    store_tok = pltpu.make_async_copy(tok_buf, prompt_rows(t), local_sem.at[1])
    store_tok.start()

    def store_shard(m):
        dst = weights.at[pl.ds(row_of(column * tp_size + t, m), kv_rows)]
        return pltpu.make_async_copy(shard_buf.at[pl.ds(m * kv_rows, kv_rows)], dst, local_sem.at[2 + m])

    @pl.when(plane == t)
    def _():
        for m in range(pieces):
            store_shard(m).start()

    for n in range(count):
        if n + LEAD < count:
            source_step(0, n + LEAD)
            source_step(1, n + LEAD)
        relay_step(0, n)
        relay_step(1, n)
        if n == Y_LAG:
            recv_wait(prompt_rows(other), tok_recv.at[0])
            remote(prompt_rows(other), prompt_rows(other), tok_send.at[2], tok_recv.at[2], r, partner).start()
        if n >= Y_LAG:
            y_step(n - Y_LAG)
    for n in range(count - Y_LAG, count):
        y_step(n)

    quarter = count * kv_rows
    recv_wait(prompt_rows(partner), tok_recv.at[1])
    recv_wait(prompt_rows((partner + half) % tp_size), tok_recv.at[2])
    for d in range(1, columns):
        recv_wait(weights.at[pl.ds(0, 2 * quarter)], x_recv.at[d - 1])
        send_wait(weights.at[pl.ds(0, 2 * quarter)], x_send.at[d - 1])
    send_wait(relay, y_send.at[0])
    for slot in range(2):
        for way, go in enumerate(ups(slot)):
            @pl.when(go)
            def _():
                send_wait(relay, z_send.at[slot, way])

    @pl.when(jnp.logical_not(handler))
    def _():
        send_wait(shard, part_send.at[0])

    for i in range(3):
        send_wait(tok, tok_send.at[i])
    store_tok.wait()

    @pl.when(plane == t)
    def _():
        for m in range(pieces):
            store_shard(m).wait()


def gather(shard, tok, q_rows, kv_rows):
    rep_size, tp_size = lax.axis_size("rep"), lax.axis_size("tp")
    columns = rep_size // tp_size
    width = shard.shape[1]
    pieces = q_rows // kv_rows + 2
    count = 2 * pieces
    hbm = pl.BlockSpec(memory_space=pltpu.HBM)
    dma = pltpu.SemaphoreType.DMA
    weights, prompts, _ = pl.pallas_call(
        functools.partial(gather_kernel, rep_size, tp_size, q_rows, kv_rows),
        out_shape=(
            jax.ShapeDtypeStruct((rep_size * shard.shape[0], width), shard.dtype),
            jax.ShapeDtypeStruct((tp_size * tok.shape[0], width), tok.dtype),
            jax.ShapeDtypeStruct((count * kv_rows, width), shard.dtype),
        ),
        in_specs=[hbm, hbm],
        out_specs=(hbm, hbm, hbm),
        scratch_shapes=[
            pltpu.VMEM(shard.shape, shard.dtype),
            pltpu.VMEM(tok.shape, tok.dtype),
            dma((2 + pieces,)),
            dma((1,)), dma((pieces,)),
            dma((2, 2)), dma((2, count)),
            dma((1,)), dma((count,)),
            dma((columns - 1,)), dma((columns - 1,)),
            dma((3,)), dma((3,)),
        ],
        compiler_params=pltpu.CompilerParams(has_side_effects=True, vmem_limit_bytes=16 * 2**20),
    )(shard, tok)
    return weights, prompts


def shards(q_weight, key_projection_weight, value_projection_weight, tokens):
    shard = jnp.concatenate(
        [q_weight, key_projection_weight, value_projection_weight], 0
    ).astype(jnp.bfloat16)
    weights, prompts = gather(shard, tokens, q_weight.shape[0], key_projection_weight.shape[0])
    projected = lax.dot_general(
        prompts, weights, (((1,), (1,)), ((), ())), preferred_element_type=jnp.float32
    )
    return weights, projected.astype(jnp.bfloat16)


def solution(mesh):
    spec = P(("rep", "tp"), None)
    return jax.shard_map(
        shards, mesh=mesh, in_specs=(spec,) * 4, out_specs=(P("tp", None), P("rep", "tp")), check_vma=False
    )
```

time: 515 us -> 289 us (0.56)
  waiting for transfers between devices: 354 us -> 0 us
  Pallas kernels: 0 us -> 240 us
  blocking collectives: 91.2 us -> 0 us
  between operations: 14.2 us -> 0.68 us
  local copies, waits for them, and re-layouts: 23.1 us -> 17.6 us
    all_gather x2 -> x0, waiting for transfers between devices: 353 us -> none  [the longest x1 353 us: shards(): segment = lax.all_gather(column_block, 'rep', axis=1, tiled=True)]
    pallas_call x0 -> x1, Pallas kernels: none -> 240 us  [gather(): pl.pallas_call(functools.partial(gather_kernel, rep_size, tp_size, q_rows...]
    all_to_all x2 -> x0, blocking collectives: 91.2 us -> none  [the longest x1 57 us: shards(): lax.all_to_all(split_cols, 'rep', split_axis=1, concat_axis=1, tiled=True)]
    unnamed x7 -> x9, local copies, waits for them, and re-layouts: 22.4 us -> 17.6 us
  transfers between devices with their start and end apart: 2 -> 0, of which waited for: 1 -> 0; matrix products, arithmetic and copies ran while one was open for 1% -> 0% of each run, Pallas kernels for 0% -> 0%
where the time goes in v1:
time: 289 us; the launch traced here: 288 us
  Pallas kernels  240 us (83%)
  matrix products  25.3 us (9%)
  local copies, waits for them, and re-layouts  17.6 us (6%)
  other arithmetic  4.68 us (2%)
    pallas_call x1, Pallas kernels, gather(): pl.pallas_call(functools.partial(gather_kernel, rep_size, tp_size, q_rows...  240 us
    dot_general x1, matrix products, shards(): lax.dot_general(prompts, weights, (((1,), (1,)), ((), ())), preferred_ele...  25.3 us
    unnamed x9, local copies, waits for them, and re-layouts  17.6 us

profile of v1, /device:TPU:5, one launch (start us, length us, event | category | flops | bytes accessed | tf_op | source)
XLA Modules:
  0.0 288.4 jit_solution(3167248960063898248)
XLA Ops:
  0.6 1.1 convert.10
  1.8 1.1 convert.11
  2.9 0.0 copy-start.2
  2.9 2.3 convert.9
  5.2 0.1 pad_maximum_fusion.shard
  5.3 0.3 copy-done.2
  5.6 240.1 %shard_map.59 = (bf16[1792,5120]{1,0:T(8,128)(2,1)S(1)}, bf16[1024,5120]{1,0:T(8,128)(2,1)S(1)}, bf16[448,5120]{1,0:T(8,128)(2,1)}) custom-call(bf16[224,5120]{1,0:T(8,128)(2,1)S(1)} %pad_maximum_fusion.shard, bf16[256,5120]{1,0:T(8,128)(2,1)S(1)} %copy-done.2), custom_call_target="tpu_custom_call" | custom-call | tf_op jit(solution)/shard_map/pallas_call | solution.py:205
  245.8 0.0 copy-start
  245.8 6.7 %copy-done = bf16[1792,5120]{1,0:T(8,128)(2,1)} copy-done((bf16[1792,5120]{1,0:T(8,128)(2,1)}, bf16[1792,5120]{1,0:T(8,128)(2,1)S(1)}, u32[]{:S(2)}) %copy-start) | copy-done | bytes 18350104
  252.4 0.0 copy-start.3
  252.4 4.0 %copy-done.3 = bf16[1024,5120]{1,0:T(8,128)(2,1)} copy-done((bf16[1024,5120]{1,0:T(8,128)(2,1)}, bf16[1024,5120]{1,0:T(8,128)(2,1)S(1)}, u32[]{:S(2)}) %copy-start.3) | copy-done | bytes 10485784
  256.4 0.0 copy-start.1
  256.4 25.3 %convolution_convert_fusion = bf16[1024,1792]{1,0:T(8,128)(2,1)} fusion(bf16[1024,5120]{1,0:T(8,128)(2,1)} %copy-done.3, bf16[1792,5120]{1,0:T(8,128)(2,1)} %copy-done), kind=kOutput, calls=%fused_computation | convolution fusion | flops 18792316928 | bytes 32505856 | tf_op jit(solution)/shard_map/dot_general | solution.py:234
  281.7 0.0 copy-done.1
  281.7 6.7 %copy.7 = bf16[1792,5120]{1,0:T(8,128)(2,1)} copy(bf16[1792,5120]{1,0:T(8,128)(2,1)S(1)} %copy-done.1) | data formatting | bytes 36700160
Async XLA Ops:
  2.9 2.7 copy-start.2
  245.8 6.7 %copy-start = (bf16[1792,5120]{1,0:T(8,128)(2,1)}, bf16[1792,5120]{1,0:T(8,128)(2,1)S(1)}, u32[]{:S(2)}) copy-start(bf16[1792,5120]{1,0:T(8,128)(2,1)S(1)} %get-tuple-element.8) | copy-start | bytes 55050244
  252.4 4.0 %copy-start.3 = (bf16[1024,5120]{1,0:T(8,128)(2,1)}, bf16[1024,5120]{1,0:T(8,128)(2,1)S(1)}, u32[]{:S(2)}) copy-start(bf16[1024,5120]{1,0:T(8,128)(2,1)S(1)} %get-tuple-element.5) | copy-start | bytes 31457284
  256.4 25.3 %copy-start.1 = (bf16[1792,5120]{1,0:T(8,128)(2,1)S(1)}, bf16[1792,5120]{1,0:T(8,128)(2,1)}, u32[]{:S(2)}) copy-start(bf16[1792,5120]{1,0:T(8,128)(2,1)} %copy-done) | copy-start | bytes 55050244

commit v2 on v1

v2 whole, which is shorter than its diff:
```python
import functools

import jax
import jax.numpy as jnp
from jax import lax
from jax.experimental import pallas as pl
from jax.experimental.pallas import tpu as pltpu
from jax.sharding import PartitionSpec as P

MESH = pl.DeviceIdType.MESH
LEAD = 3
Y_LAG = 3
TOK_AT = 11
LATE_FIRST = 1
LATE_EVERY = 3


def gather_kernel(
    rep_size, tp_size, q_rows, kv_rows,
    shard, tok, weights, projected,
    prompts, relay, shard_buf, block_buf, result_buf, local_sem, block_sem, result_sem,
    part_send, part_recv, z_send, z_recv, y_send, y_recv, x_send, x_recv, tok_send, tok_recv,
):
    planes = tp_size
    columns = rep_size // planes
    half = tp_size // 2
    r, t = lax.axis_index("rep"), lax.axis_index("tp")
    plane, column = r // columns, r % columns
    side, core = t // 2, t % 2
    other = (t + half) % tp_size
    partner = t + 1 - 2 * core
    q_chunks = q_rows // kv_rows
    pieces = q_chunks + 2
    count = 2 * pieces
    shards_in_plane = tp_size * columns
    ranks = (t, other)
    order = (q_chunks, q_chunks + 1) + tuple(range(q_chunks))

    def row_of(index, m):
        if m < q_chunks:
            return pl.multiple_of(index * q_rows + m * kv_rows, 8)
        base = shards_in_plane * (q_rows + (m - q_chunks) * kv_rows)
        return pl.multiple_of(base + index * kv_rows, 8)

    def in_weights(at_side, n):
        of_core = core if n < pieces else 1 - core
        return weights.at[pl.ds(row_of(column * tp_size + at_side * 2 + of_core, order[n % pieces]), kv_rows)]

    def in_relay(n):
        return relay.at[pl.ds(n * kv_rows, kv_rows)]

    def in_shard(n):
        return shard.at[pl.ds(order[n] * kv_rows, kv_rows)]

    def place(slot, n):
        return in_weights(side, n) if slot == 0 else in_relay(n)

    def remote(src, dst, send, recv, to_rep, to_tp):
        return pltpu.make_async_remote_copy(
            src_ref=src, dst_ref=dst, send_sem=send, recv_sem=recv,
            device_id=(to_rep, to_tp), device_id_type=MESH,
        )

    def ups(slot):
        k = ranks[slot]
        return (plane >= k) & (plane < planes - 1), (plane <= k) & (plane > 0)

    def x_sends(n, src, dst):
        kind = 0 if n % pieces < 2 else 1
        for d in range(1, columns):
            to = plane * columns + (column + d) % columns
            remote(src, dst, x_send.at[d - 1], x_recv.at[d - 1, kind], to, t).start()

    def forward(slot, n, src, from_source=False):
        up, down = ups(slot)
        if from_source:
            up, down = up & (plane != planes - 2), down & (plane != 1)
        dst = place(slot, n)

        @pl.when(up)
        def _():
            remote(src, dst, z_send.at[slot, 0], z_recv.at[slot, n], r + columns, t).start()

        @pl.when(down)
        def _():
            remote(src, dst, z_send.at[slot, 1], z_recv.at[slot, n], r - columns, t).start()

        if slot == 0:
            x_sends(n, src, dst)
        else:
            remote(src, in_weights(side, n), y_send.at[0], y_recv.at[n], r, other).start()

    def recv_wait(dst, sem):
        remote(dst, dst, x_send.at[0], sem, r, partner).wait_recv()

    def send_wait(src, sem):
        remote(src, src, sem, x_recv.at[0, 0], r, partner).wait_send()

    def source_step(slot, n):
        @pl.when(plane == ranks[slot])
        def _():
            if n < pieces:
                forward(slot, n, in_shard(n), True)
            else:
                recv_wait(place(slot, n), part_recv.at[n - pieces])
                forward(slot, n, place(slot, n), True)

    def late_step(slot, n):
        up, down = ups(slot)
        src, dst = in_shard(n) if n < pieces else place(slot, n), place(slot, n)

        @pl.when((plane == ranks[slot]) & up & (plane == planes - 2))
        def _():
            remote(src, dst, z_send.at[slot, 0], z_recv.at[slot, n], r + columns, t).start()

        @pl.when((plane == ranks[slot]) & down & (plane == 1))
        def _():
            remote(src, dst, z_send.at[slot, 1], z_recv.at[slot, n], r - columns, t).start()

    def relay_step(slot, n):
        @pl.when(plane != ranks[slot])
        def _():
            recv_wait(place(slot, n), z_recv.at[slot, n])
            forward(slot, n, place(slot, n))

    def y_step(n):
        block = in_weights(1 - side, n)
        recv_wait(block, y_recv.at[n])
        x_sends(n, block, block)

    rows = tok.shape[0]

    def prompt_rows(rank):
        return prompts.at[pl.ds(pl.multiple_of(rank * rows, 8), rows)]

    handler = core == plane % 2
    load_shard = pltpu.make_async_copy(shard, shard_buf, local_sem.at[0])
    load_tok = pltpu.make_async_copy(tok, prompt_rows(t), local_sem.at[1])
    load_shard.start()
    load_tok.start()

    @pl.when(jnp.logical_not(handler))
    def _():
        for m in range(pieces):
            @pl.when(side == plane // 2)
            def _():
                dst = weights.at[pl.ds(row_of(column * tp_size + t, order[m]), kv_rows)]
                remote(in_shard(m), dst, part_send.at[0], part_recv.at[m], r, partner).start()

            @pl.when(side != plane // 2)
            def _():
                remote(in_shard(m), in_relay(pieces + m), part_send.at[0], part_recv.at[m], r, partner).start()

    remote(tok, prompt_rows(t), tok_send.at[1], tok_recv.at[1], r, partner).start()

    for n in range(LEAD):
        source_step(0, n)
        source_step(1, n)

    load_shard.wait()
    load_tok.wait()

    def store_shard(m):
        dst = weights.at[pl.ds(row_of(column * tp_size + t, m), kv_rows)]
        return pltpu.make_async_copy(shard_buf.at[pl.ds(m * kv_rows, kv_rows)], dst, local_sem.at[2 + m])

    @pl.when(plane == t)
    def _():
        for m in range(pieces):
            store_shard(m).start()

    late = 0
    for n in range(LATE_FIRST):
        late_step(0, n)
        late_step(1, n)
        late += 1
    for n in range(count):
        if n % LATE_EVERY == LATE_EVERY - 1 and late < count:
            late_step(0, late)
            late_step(1, late)
            late += 1
        if n + LEAD < count:
            source_step(0, n + LEAD)
            source_step(1, n + LEAD)
        relay_step(0, n)
        relay_step(1, n)
        if n == TOK_AT:
            remote(tok, prompt_rows(t), tok_send.at[0], tok_recv.at[0], r, other).start()
        if n >= Y_LAG:
            y_step(n - Y_LAG)
    for n in range(late, count):
        late_step(0, n)
        late_step(1, n)
    for n in range(count - Y_LAG, count):
        y_step(n)
    recv_wait(prompt_rows(other), tok_recv.at[0])
    remote(prompt_rows(other), prompt_rows(other), tok_send.at[2], tok_recv.at[2], r, partner).start()

    recv_wait(prompt_rows(partner), tok_recv.at[1])
    recv_wait(prompt_rows((partner + half) % tp_size), tok_recv.at[2])

    @pl.when(plane == t)
    def _():
        for m in range(pieces):
            store_shard(m).wait()

    block = block_buf.shape[1]
    token_tile = min(256, prompts.shape[0])
    quarter = count * kv_rows
    own = tp_size * q_rows
    firsts = [-(-(c * own) // block) for c in range(columns)]
    early = min((c + 1) * own // block - firsts[c] for c in range(columns))
    early = max(early, 0)
    q_blocks = columns * own // block
    first = (column * own + block - 1) // block

    def load_block(index, at):
        src = weights.at[pl.ds(pl.multiple_of(index * block, block), block)]
        return pltpu.make_async_copy(src, block_buf.at[at], block_sem.at[at])

    def store_block(index, at):
        dst = projected.at[:, pl.ds(pl.multiple_of(index * block, block), block)]
        return pltpu.make_async_copy(result_buf.at[at], dst, result_sem.at[at])

    here = [first + i for i in range(early)] + [q_blocks, q_blocks + 1]
    last = [jnp.where(i >= first, i + early, i) for i in range(q_blocks - early)]
    blocks = here + last

    def multiply(i):
        at = i % 2
        load_block(blocks[i], at).wait()
        if i >= 2:
            store_block(blocks[i - 2], at).wait()

        @pl.loop(0, prompts.shape[0] // token_tile)
        def _(tile):
            at_rows = pl.ds(pl.multiple_of(tile * token_tile, token_tile), token_tile)
            result_buf[at, at_rows, :] = lax.dot_general(
                prompts[at_rows, :], block_buf[at], (((1,), (1,)), ((), ())),
                preferred_element_type=jnp.float32,
            ).astype(result_buf.dtype)

        store_block(blocks[i], at).start()

    kv_part = 2 * 2 * 2 * kv_rows
    if early:
        load_block(blocks[0], 0).start()
    for d in range(1, columns):
        recv_wait(weights.at[pl.ds(0, kv_part)], x_recv.at[d - 1, 0])
    if not early:
        load_block(blocks[0], 0).start()
    for i in range(len(here)):
        if i + 1 < len(here):
            load_block(blocks[i + 1], (i + 1) % 2).start()
        multiply(i)
    for d in range(1, columns):
        recv_wait(weights.at[pl.ds(0, 2 * quarter - kv_part)], x_recv.at[d - 1, 1])
    load_block(blocks[len(here)], len(here) % 2).start()
    for i in range(len(here), len(blocks)):
        if i + 1 < len(blocks):
            load_block(blocks[i + 1], (i + 1) % 2).start()
        multiply(i)
    for i in range(len(blocks) - 2, len(blocks)):
        store_block(blocks[i], i % 2).wait()

    for d in range(1, columns):
        send_wait(weights.at[pl.ds(0, 2 * quarter)], x_send.at[d - 1])
    send_wait(relay, y_send.at[0])
    for slot in range(2):
        for way, go in enumerate(ups(slot)):
            @pl.when(go)
            def _():
                send_wait(relay, z_send.at[slot, way])

    @pl.when(jnp.logical_not(handler))
    def _():
        send_wait(shard, part_send.at[0])

    for i in range(3):
        send_wait(tok, tok_send.at[i])


def gather(shard, tok, q_rows, kv_rows):
    rep_size, tp_size = lax.axis_size("rep"), lax.axis_size("tp")
    columns = rep_size // tp_size
    width = shard.shape[1]
    pieces = q_rows // kv_rows + 2
    count = 2 * pieces
    hbm = pl.BlockSpec(memory_space=pltpu.HBM)
    dma = pltpu.SemaphoreType.DMA
    block = columns * tp_size * kv_rows
    tokens = tp_size * tok.shape[0]
    total = rep_size * shard.shape[0]
    return pl.pallas_call(
        functools.partial(gather_kernel, rep_size, tp_size, q_rows, kv_rows),
        out_shape=(
            jax.ShapeDtypeStruct((total, width), shard.dtype),
            jax.ShapeDtypeStruct((tokens, total), tok.dtype),
        ),
        in_specs=[hbm, hbm],
        out_specs=(hbm, hbm),
        scratch_shapes=[
            pltpu.VMEM((tokens, width), tok.dtype),
            pltpu.VMEM((count * kv_rows, width), shard.dtype),
            pltpu.VMEM(shard.shape, shard.dtype),
            pltpu.VMEM((2, block, width), shard.dtype),
            pltpu.VMEM((2, tokens, block), tok.dtype),
            dma((2 + pieces,)), dma((2,)), dma((2,)),
            dma((1,)), dma((pieces,)),
            dma((2, 2)), dma((2, count)),
            dma((1,)), dma((count,)),
            dma((columns - 1,)), dma((columns - 1, 2)),
            dma((3,)), dma((3,)),
        ],
        compiler_params=pltpu.CompilerParams(has_side_effects=True, vmem_limit_bytes=26 * 2**20),
    )(shard, tok)


def shards(q_weight, key_projection_weight, value_projection_weight, tokens):
    shard = jnp.concatenate(
        [q_weight, key_projection_weight, value_projection_weight], 0
    ).astype(jnp.bfloat16)
    return gather(shard, tokens, q_weight.shape[0], key_projection_weight.shape[0])


def solution(mesh):
    spec = P(("rep", "tp"), None)
    return jax.shard_map(
        shards, mesh=mesh, in_specs=(spec,) * 4, out_specs=(P("tp", None), P("rep", "tp")), check_vma=False
    )
```

time: 289 us -> 251 us (0.87)
  matrix products: 25.3 us -> 0 us
  local copies, waits for them, and re-layouts: 17.6 us -> 8.79 us
  Pallas kernels: 240 us -> 236 us
    dot_general x1 -> x0, matrix products: 25.3 us -> none  [shards(): lax.dot_general(prompts, weights, (((1,), (1,)), ((), ())), preferred_ele...]
    unnamed x9 -> x4, local copies, waits for them, and re-layouts: 17.6 us -> 8.79 us
    pallas_call x1, Pallas kernels: 240 us -> 236 us  [gather(): pl.pallas_call(functools.partial(gather_kernel, rep_size, tp_size, q_rows...]
where the time goes in v2:
time: 251 us; the launch traced here: 250 us
  Pallas kernels  236 us (94%)
  local copies, waits for them, and re-layouts  8.79 us (4%)
  other arithmetic  4.68 us (2%)
    pallas_call x1, Pallas kernels, gather(): pl.pallas_call(functools.partial(gather_kernel, rep_size, tp_size, q_rows...  236 us
    unnamed x4, local copies, waits for them, and re-layouts  8.79 us

profile of v2, /device:TPU:5, one launch (start us, length us, event | category | flops | bytes accessed | tf_op | source)
XLA Modules:
  0.0 250.4 jit_solution(6737418093134146863)
XLA Ops:
  0.6 1.1 convert.10
  1.8 1.1 convert.11
  2.9 0.0 copy-start
  2.9 2.3 convert.9
  5.2 0.1 pad_maximum_fusion.shard
  5.3 0.3 copy-done
  5.6 236.2 %shard_map.59 = (bf16[1792,5120]{1,0:T(8,128)(2,1)S(1)}, bf16[1024,1792]{1,0:T(8,128)(2,1)S(1)}) custom-call(bf16[224,5120]{1,0:T(8,128)(2,1)S(1)} %pad_maximum_fusion.shard, bf16[256,5120]{1,0:T(8,128)(2,1)S(1)} %copy-done), custom_call_target="tpu_custom_call" | custom-call | tf_op jit(solution)/shard_map/pallas_call | solution.py:294
  241.8 6.7 %copy.8 = bf16[1792,5120]{1,0:T(8,128)(2,1)} copy(bf16[1792,5120]{1,0:T(8,128)(2,1)S(1)} %get-tuple-element.4) | data formatting | bytes 36700160
  248.5 1.8 copy.9
Async XLA Ops:
  2.9 2.7 %copy-start = (bf16[256,5120]{1,0:T(8,128)(2,1)S(1)}, bf16[256,5120]{1,0:T(8,128)(2,1)}, u32[]{:S(2)}) copy-start(bf16[256,5120]{1,0:T(8,128)(2,1)} %tok.1) | copy-start | bytes 7864324

commit v3 on v2

--- a/solution.py
+++ b/solution.py
@@ -9,10 +9,10 @@
 
 MESH = pl.DeviceIdType.MESH
 LEAD = 3
-Y_LAG = 3
+Y_LAG = 2
 TOK_AT = 11
 LATE_FIRST = 1
-LATE_EVERY = 3
+LATE_EVERY = 2
 
 
 def gather_kernel(
@@ -65,8 +65,8 @@
         k = ranks[slot]
         return (plane >= k) & (plane < planes - 1), (plane <= k) & (plane > 0)
 
-    def x_sends(n, src, dst):
-        kind = 0 if n % pieces < 2 else 1
+    def x_sends(n, src, dst, which):
+        kind = 0 if n % pieces < 2 else 1 + which
         for d in range(1, columns):
             to = plane * columns + (column + d) % columns
             remote(src, dst, x_send.at[d - 1], x_recv.at[d - 1, kind], to, t).start()
@@ -86,7 +86,7 @@
             remote(src, dst, z_send.at[slot, 1], z_recv.at[slot, n], r - columns, t).start()
 
         if slot == 0:
-            x_sends(n, src, dst)
+            x_sends(n, src, dst, 0)
         else:
             remote(src, in_weights(side, n), y_send.at[0], y_recv.at[n], r, other).start()
 
@@ -126,7 +126,7 @@
     def y_step(n):
         block = in_weights(1 - side, n)
         recv_wait(block, y_recv.at[n])
-        x_sends(n, block, block)
+        x_sends(n, block, block, 1)
 
     rows = tok.shape[0]
 
@@ -223,7 +223,16 @@
         return pltpu.make_async_copy(result_buf.at[at], dst, result_sem.at[at])
 
     here = [first + i for i in range(early)] + [q_blocks, q_blocks + 1]
-    last = [jnp.where(i >= first, i + early, i) for i in range(q_blocks - early)]
+    left = q_blocks - early
+    places = [jnp.where(side == 0, i, left - 1 - i) for i in range(left)]
+    last = [jnp.where(i >= first, i + early, i) for i in places]
+    alone = True
+    for c in range(columns):
+        for s in range(2):
+            i = s * (left - 1)
+            low = (i + early if i >= firsts[c] else i) * block
+            for part in range(low // (2 * q_rows), (low + block - 1) // (2 * q_rows) + 1):
+                alone = alone and (part // 2 == c or part % 2 == s)
     blocks = here + last
 
     def multiply(i):
@@ -253,13 +262,18 @@
         if i + 1 < len(here):
             load_block(blocks[i + 1], (i + 1) % 2).start()
         multiply(i)
-    for d in range(1, columns):
-        recv_wait(weights.at[pl.ds(0, 2 * quarter - kv_part)], x_recv.at[d - 1, 1])
-    load_block(blocks[len(here)], len(here) % 2).start()
-    for i in range(len(here), len(blocks)):
-        if i + 1 < len(blocks):
-            load_block(blocks[i + 1], (i + 1) % 2).start()
-        multiply(i)
+    done = len(here)
+    for which in (1, 2):
+        for d in range(1, columns):
+            recv_wait(weights.at[pl.ds(0, quarter - kv_part // 2)], x_recv.at[d - 1, which])
+        stop = len(blocks) if which == 2 else done + int(alone)
+        for i in range(done, stop):
+            if i == done:
+                load_block(blocks[i], i % 2).start()
+            if i + 1 < stop:
+                load_block(blocks[i + 1], (i + 1) % 2).start()
+            multiply(i)
+        done = stop
     for i in range(len(blocks) - 2, len(blocks)):
         store_block(blocks[i], i % 2).wait()
 
@@ -309,7 +323,7 @@
             dma((1,)), dma((pieces,)),
             dma((2, 2)), dma((2, count)),
             dma((1,)), dma((count,)),
-            dma((columns - 1,)), dma((columns - 1, 2)),
+            dma((columns - 1,)), dma((columns - 1, 3)),
             dma((3,)), dma((3,)),
         ],
         compiler_params=pltpu.CompilerParams(has_side_effects=True, vmem_limit_bytes=26 * 2**20),

time: 251 us -> 247 us (0.984)
  Pallas kernels: 236 us -> 233 us
    pallas_call x1, Pallas kernels: 236 us -> 233 us  [gather(): pl.pallas_call(functools.partial(gather_kernel, rep_size, tp_size, q_rows...]
where the time goes in v3:
time: 247 us
  Pallas kernels  233 us (94%)
  local copies, waits for them, and re-layouts  8.79 us (4%)
  other arithmetic  4.68 us (2%)
    pallas_call x1, Pallas kernels, gather(): pl.pallas_call(functools.partial(gather_kernel, rep_size, tp_size, q_rows...  233 us
    unnamed x4, local copies, waits for them, and re-layouts  8.79 us

profile of v3, /device:TPU:5, one launch (start us, length us, event | category | flops | bytes accessed | tf_op | source)
XLA Modules:
  0.0 246.6 jit_solution(8338468079573788930)
XLA Ops:
  0.6 1.1 convert.10
  1.8 1.1 convert.11
  2.9 0.0 copy-start
  2.9 2.3 convert.9
  5.2 0.1 pad_maximum_fusion.shard
  5.3 0.3 copy-done
  5.6 232.5 %shard_map.59 = (bf16[1792,5120]{1,0:T(8,128)(2,1)S(1)}, bf16[1024,1792]{1,0:T(8,128)(2,1)S(1)}) custom-call(bf16[224,5120]{1,0:T(8,128)(2,1)S(1)} %pad_maximum_fusion.shard, bf16[256,5120]{1,0:T(8,128)(2,1)S(1)} %copy-done), custom_call_target="tpu_custom_call" | custom-call | tf_op jit(solution)/shard_map/pallas_call | solution.py:308
  238.1 6.7 %copy.8 = bf16[1792,5120]{1,0:T(8,128)(2,1)} copy(bf16[1792,5120]{1,0:T(8,128)(2,1)S(1)} %get-tuple-element.4) | data formatting | bytes 36700160
  244.8 1.8 copy.9
Async XLA Ops:
  2.9 2.7 %copy-start = (bf16[256,5120]{1,0:T(8,128)(2,1)S(1)}, bf16[256,5120]{1,0:T(8,128)(2,1)}, u32[]{:S(2)}) copy-start(bf16[256,5120]{1,0:T(8,128)(2,1)} %tok.1) | copy-start | bytes 7864324
